TPU v7x, 32 devices: a whole 2x2x4 slice. The times are simulated.
32 devices in a mesh: seq: 4 (over z), head: 4 (over y, x), batch: 2 (over core).
Axes of the slice: x: 2, y: 2, z: 4, core: 2. Of those that a mesh axis runs over, the one named last changes fastest.
Arguments:
- ssm_input: bfloat16 [16384, 5120], P(('batch', 'seq'), 'head'), parts along dimension 0, may hold values from -500 to 500
- gate_input: bfloat16 [16384, 5120], P(('batch', 'seq'), 'head'), parts along dimension 0, may hold values from -6 to 6
- b_proj: bfloat16 [16384, 1024], P(('batch', 'seq')), parts along dimension 0, may hold values from -2 to 2
- c_proj: bfloat16 [16384, 1024], P(('batch', 'seq')), parts along dimension 0, may hold values from -2 to 2
- step_size: float32 [80, 16384], P('head', ('batch', 'seq')), parts along dimension 1, may hold values from 0.02 to 0.2
- log_decay: float32 [80, 16384], P('head', ('batch', 'seq')), parts along dimension 1, may hold values from -1.5 to 0, as said below
- skip_gain: float32 [80], P('head'), may hold values from 0.5 to 1.5
- norm_gain: float32 [5120], replicated, may hold values from 0.1 to 1.9
- out_weight: bfloat16 [5120, 2560], P('head'), may hold values from -0.078125 to 0.078125
Outputs:
- layer_out: bfloat16 [16384, 2560], P(('batch', 'seq', 'head')), parts along dimension 0
There are 2 independent parts, one for each index of `batch`. A program takes and returns all parts, laid end to end along the dimension named above; an argument that names none is the same for every part. Nothing has to cross between parts.
Inputs may be any that keep to these rules, and one draw needn't show every extreme that they name: `log_decay`: negative.
All inputs are finite; a program needn't handle non-finite values.
Results may differ from a plain program's by a relative error of at most 0.018.
Values may be sent and summed in bfloat16 or wider, within the bound.
A program may use at most 192 MiB of HBM per device.

v0:
```python
import functools
import jax
import jax.numpy as jnp
from jax import lax
from jax.experimental import pallas as pl
from jax.experimental.pallas import tpu as pltpu
from jax.sharding import PartitionSpec as P

HEAD_COUNT = 80
HEAD_DIM = 64
STATE = 128
GROUPS = 8
BLOCK = 256
LANES = 128
epsilon = 1e-05
HIGHEST = lax.Precision.HIGHEST
F32 = jnp.float32
BF16 = jnp.bfloat16


def dot(a, b, ca, cb, precision=None):
    return lax.dot_general(
        a, b, (((ca,), (cb,)), ((), ())), precision=precision, preferred_element_type=F32
    )


def iotas(rows, columns):
    return (
        lax.broadcasted_iota(jnp.int32, (rows, columns), 0),
        lax.broadcasted_iota(jnp.int32, (rows, columns), 1),
    )


def lower_ones():
    t, s = iotas(BLOCK, BLOCK)
    return jnp.where(s <= t, 1.0, 0.0).astype(F32)


def identity():
    t, s = iotas(BLOCK, BLOCK)
    return jnp.where(s == t, 1.0, 0.0).astype(F32)


def pieces(channels, repeats):
    found = []
    for start in range(0, channels, LANES):
        width = min(LANES, channels - start)
        heads = [start // HEAD_DIM + i for i in range(width // HEAD_DIM)]
        found.append((start, width, heads, heads[0] // repeats))
    return found


def spread(columns, heads, width):
    first = jnp.broadcast_to(columns[:, heads[0] : heads[0] + 1], (BLOCK, width))
    if len(heads) == 1:
        return first
    second = jnp.broadcast_to(columns[:, heads[1] : heads[1] + 1], (BLOCK, width))
    lane = iotas(BLOCK, width)[1]
    return jnp.where(lane < HEAD_DIM, first, second)


def state_kernel(
    repeats, at_ref, x_ref, b_ref, step_ref, log_ref, prefix_ref, base_ref, total_ref, all_ref, s_ref, l_ref
):
    k = pl.program_id(0)
    channels = x_ref.shape[1]

    @pl.when(k == 0)
    def _():
        s_ref[...] = jnp.zeros_like(s_ref)
        l_ref[...] = jnp.zeros_like(l_ref)

    columns = dot(lower_ones(), log_ref[...], 1, 1, HIGHEST)
    steps = dot(identity(), step_ref[...], 1, 1, HIGHEST)
    base_ref[0] = l_ref[...]
    prefix_ref[0] = s_ref[...].astype(BF16)
    for start, width, heads, group in pieces(channels, repeats):
        lanes = pl.ds(start, width)
        cum = spread(columns, heads, width)
        last = cum[BLOCK - 1 : BLOCK, :]
        weighted = (
            x_ref[:, lanes].astype(F32) * (jnp.exp(last - cum) * spread(steps, heads, width))
        ).astype(BF16)
        new = dot(b_ref[:, group * STATE : (group + 1) * STATE], weighted, 0, 0)
        s_ref[:, lanes] = jnp.exp(last) * s_ref[:, lanes] + new
        l_ref[:, lanes] = l_ref[:, lanes] + last
    total_ref[...] = s_ref[...]
    all_ref[...] = jnp.exp(l_ref[...])


def within_kernel(
    repeats, at_ref, x_ref, b_ref, c_ref, step_ref, log_ref, skip_ref, prefix_ref, y_ref
):
    channels = x_ref.shape[1]
    half = BLOCK // 2
    lower = lower_ones()
    columns = dot(lower, log_ref[...], 1, 1, HIGHEST)
    rows = dot(log_ref[...], lower, 1, 1, HIGHEST) - jnp.log(step_ref[...])
    scores = {}
    for start, width, heads, group in pieces(channels, repeats):
        lanes = pl.ds(start, width)
        c_here = c_ref[:, group * STATE : (group + 1) * STATE]
        if group not in scores:
            full = dot(c_here, b_ref[:, group * STATE : (group + 1) * STATE], 1, 1)
            scores[group] = full * lower
        x_here = x_ref[:, lanes]
        lane = iotas(BLOCK, width)[1]
        top, bottom = 0.0, 0.0
        for i, head in enumerate(heads):
            kept = (lane >= i * HEAD_DIM) & (lane < (i + 1) * HEAD_DIM)
            x_head = x_here if len(heads) == 1 else jnp.where(kept, x_here, jnp.zeros_like(x_here))
            column, row = columns[:, head : head + 1], rows[head : head + 1, :]
            w_top = scores[group][:half, :half] * jnp.exp(
                jnp.minimum(column[:half] - row[:, :half], 0.0)
            )
            w_bottom = scores[group][half:] * jnp.exp(jnp.minimum(column[half:] - row, 0.0))
            top = top + dot(w_top.astype(BF16), x_head[:half], 1, 0)
            bottom = bottom + dot(w_bottom.astype(BF16), x_head, 1, 0)
        across = jnp.exp(spread(columns, heads, width)) * dot(c_here, prefix_ref[0, :, lanes], 1, 0)
        rest = across + skip_ref[:, lanes] * x_here.astype(F32)
        y_ref[:half, lanes] = (top + rest[:half]).astype(BF16)
        y_ref[half:, lanes] = (bottom + rest[half:]).astype(BF16)


def finish_kernel(
    repeats, at_ref, y_ref, gate_ref, c_ref, log_ref, base_ref, in_ref, gain_ref, w_ref, out_ref, sq_ref, g_ref
):
    channels = y_ref.shape[1]
    columns = dot(lower_ones(), log_ref[...], 1, 1, HIGHEST)
    squares = jnp.zeros((8, BLOCK), F32)
    for start, width, heads, group in pieces(channels, repeats):
        lanes = pl.ds(start, width)
        grow = jnp.exp(spread(columns, heads, width) + base_ref[0, 0:1, lanes])
        across = grow * dot(c_ref[:, group * STATE : (group + 1) * STATE], in_ref[:, lanes], 1, 0)
        gate = gate_ref[:, lanes].astype(F32)
        gated = (y_ref[:, lanes].astype(F32) + across) * (gate / (1.0 + jnp.exp(-gate)))
        squares = squares + dot(jnp.ones((8, width), BF16), (gated * gated).astype(BF16), 1, 1)
        g_ref[:, lanes] = (gated * gain_ref[:, lanes]).astype(BF16)
    sq_ref[...] = squares
    model = w_ref.shape[1]
    tile = 512 if model % 512 == 0 else model
    for start in range(0, model, tile):
        out_ref[:, start : start + tile] = dot(
            g_ref[...], w_ref[:, start : start + tile], 1, 0
        ).astype(BF16)


def shifted(value, axis, steps):
    count = lax.axis_size(axis)
    return lax.ppermute(value, axis, [(source, source + steps) for source in range(count - steps)])


def body(
    ssm_input, gate_input, b_proj, c_proj, step_size, log_decay, skip_gain, norm_gain, out_weight
):
    tokens, channels = ssm_input.shape
    heads = step_size.shape[0]
    blocks = tokens // BLOCK
    model = out_weight.shape[1]
    per_group = HEAD_COUNT // GROUPS
    groups = max(1, heads // per_group)
    repeats = min(heads, per_group)
    head_index = lax.axis_index("head")
    at = (head_index * heads // per_group // groups).astype(jnp.int32).reshape(1)
    skip = jnp.repeat(skip_gain, HEAD_DIM)[None, :]
    gain = lax.dynamic_slice_in_dim(norm_gain, head_index * channels, channels)[None, :]
    params = pltpu.CompilerParams(
        dimension_semantics=("arbitrary",), vmem_limit_bytes=56 * 1024 * 1024
    )

    def rows_of(width):
        return pl.BlockSpec((BLOCK, width), lambda k, at: (k, 0))

    grouped = pl.BlockSpec((BLOCK, groups * STATE), lambda k, at: (k, at[0]))
    head_rows = pl.BlockSpec((heads, BLOCK), lambda k, at: (0, k))
    fixed = lambda r, c: pl.BlockSpec((r, c), lambda k, at: (0, 0))
    state_block = pl.BlockSpec((1, STATE, channels), lambda k, at: (k, 0, 0))

    prefix, base, total, decay = pl.pallas_call(
        functools.partial(state_kernel, repeats),
        grid_spec=pltpu.PrefetchScalarGridSpec(
            num_scalar_prefetch=1,
            grid=(blocks,),
            in_specs=[rows_of(channels), grouped, head_rows, head_rows],
            out_specs=[
                state_block,
                pl.BlockSpec((1, 8, channels), lambda k, at: (k, 0, 0)),
                fixed(STATE, channels),
                fixed(8, channels),
            ],
            scratch_shapes=[pltpu.VMEM((STATE, channels), F32), pltpu.VMEM((8, channels), F32)],
        ),
        out_shape=[
            jax.ShapeDtypeStruct((blocks, STATE, channels), BF16),
            jax.ShapeDtypeStruct((blocks, 8, channels), F32),
            jax.ShapeDtypeStruct((STATE, channels), F32),
            jax.ShapeDtypeStruct((8, channels), F32),
        ],
        compiler_params=params,
        name="block_states",
        cost_estimate=pl.CostEstimate(
            flops=2 * tokens * channels * STATE, bytes_accessed=tokens * channels * 4, transcendentals=0
        ),
    )(at, ssm_input, b_proj, step_size, log_decay)

    incoming = shifted(total.astype(BF16), "seq", 1)
    for _ in range(lax.axis_size("seq") - 2):
        incoming = shifted((decay[0:1] * incoming.astype(F32) + total).astype(BF16), "seq", 1)

    y = pl.pallas_call(
        functools.partial(within_kernel, repeats),
        grid_spec=pltpu.PrefetchScalarGridSpec(
            num_scalar_prefetch=1,
            grid=(blocks,),
            in_specs=[
                rows_of(channels),
                grouped,
                grouped,
                head_rows,
                head_rows,
                fixed(1, channels),
                state_block,
            ],
            out_specs=rows_of(channels),
        ),
        out_shape=jax.ShapeDtypeStruct((tokens, channels), BF16),
        compiler_params=params,
        name="within",
        cost_estimate=pl.CostEstimate(
            flops=16 * tokens * channels * BLOCK, bytes_accessed=tokens * channels * 8, transcendentals=0
        ),
    )(at, ssm_input, b_proj, c_proj, step_size, log_decay, skip, prefix)

    shares = lax.axis_size("head")
    per_share = tokens // shares
    chunks = max(1, per_share // BLOCK)
    steps = blocks // chunks
    parts, squares = [], []
    for chunk in range(chunks):
        pick = lambda d, chunk=chunk: d * chunks + chunk
        partial, square = pl.pallas_call(
            functools.partial(finish_kernel, repeats),
            grid_spec=pltpu.PrefetchScalarGridSpec(
                num_scalar_prefetch=1,
                grid=(steps,),
                in_specs=[
                    pl.BlockSpec((BLOCK, channels), lambda d, at: (pick(d), 0)),
                    pl.BlockSpec((BLOCK, channels), lambda d, at: (pick(d), 0)),
                    pl.BlockSpec((BLOCK, groups * STATE), lambda d, at: (pick(d), at[0])),
                    pl.BlockSpec((heads, BLOCK), lambda d, at: (0, pick(d))),
                    pl.BlockSpec((1, 8, channels), lambda d, at: (pick(d), 0, 0)),
                    fixed(STATE, channels),
                    fixed(1, channels),
                    fixed(channels, model),
                ],
                out_specs=[
                    pl.BlockSpec((BLOCK, model), lambda d, at: (d, 0)),
                    pl.BlockSpec((8, BLOCK), lambda d, at: (0, d)),
                ],
                scratch_shapes=[pltpu.VMEM((BLOCK, channels), BF16)],
            ),
            out_shape=[
                jax.ShapeDtypeStruct((steps * BLOCK, model), BF16),
                jax.ShapeDtypeStruct((8, steps * BLOCK), F32),
            ],
            compiler_params=params,
            name="finish",
            cost_estimate=pl.CostEstimate(
                flops=2 * steps * BLOCK * channels * model,
                bytes_accessed=steps * BLOCK * (channels * 4 + model * 2) + channels * model * 2,
                transcendentals=0,
            ),
        )(at, y, gate_input, c_proj, log_decay, base, incoming, gain, out_weight)
        parts.append(lax.psum_scatter(partial, "head", scatter_dimension=0, tiled=True))
        squares.append(square[0].reshape(shares, per_share // chunks))
    squares = lax.psum_scatter(
        jnp.concatenate(squares, axis=1), "head", scatter_dimension=0, tiled=True
    ).reshape(per_share, 1)
    scale = lax.rsqrt(squares / (HEAD_COUNT * HEAD_DIM) + epsilon)
    return (jnp.concatenate(parts, axis=0).astype(F32) * scale).astype(BF16)


def solution(mesh):
    in_specs = (
        P(("batch", "seq"), "head"),
        P(("batch", "seq"), "head"),
        P(("batch", "seq"), None),
        P(("batch", "seq"), None),
        P("head", ("batch", "seq")),
        P("head", ("batch", "seq")),
        P("head"),
        P(),
        P("head", None),
    )
    out_specs = P(("batch", "seq", "head"), None)
    return jax.shard_map(body, mesh=mesh, in_specs=in_specs, out_specs=out_specs, check_vma=False)
```

profile of v0, /device:TPU:0, one launch (start us, length us, event | category | flops | bytes accessed | tf_op | source)
XLA Modules:
  0.0 236.6 jit_solution(11020611437053981086)
XLA Ops:
  6.5 21.3 %block_states.1 = (bf16[8,128,1280]{2,1,0:T(8,128)(2,1)}, f32[8,8,1280]{2,1,0:T(8,128)}, f32[128,1280]{1,0:T(8,128)}, f32[8,1280]{1,0:T(8,128)}) custom-call(s32[1]{0:T(128)} %bitcast.at_ref, bf16[2048,1280]{1,0:T(8,128)(2,1)} %x_ref.3, bf16[2048,1024]{1,0:T(8,128)(2,1)} %b_ref.3, f32[20,2048]{1,0:T(8,128)} %step_ref.3, f32[20,2048]{1,0:T(8,128)} %log_ref.7), custom_call_target="tpu_custom_call" | custom-call | flops 671088640 | bytes 10485760 | tf_op jit(solution)/shard_map/block_states/pallas_call | solution.py:179
  27.8 1.1 convert_element_type.21
  29.0 5.0 %collective-permute-start = (bf16[128,1280]{1,0:T(8,128)(2,1)S(1)}, bf16[128,1280]{1,0:T(8,128)(2,1)S(1)}, u32[]{:S(2)}, u32[]{:S(2)}) collective-permute-start(bf16[128,1280]{1,0:T(8,128)(2,1)S(1)} %convert_element_type.21), channel_id=1, source_target_pairs={{0,8},{8,16},{16,24},{1,9},{9,17},{17,25},{2,10},{10,18},{18,26},{... | collective-permute-start | bytes 983048 | tf_op jit(solution)/shard_map/ppermute | solution.py:150
  34.0 0.8 slice_reduce_fusion
  34.8 6.1 %collective-permute-done = bf16[128,1280]{1,0:T(8,128)(2,1)S(1)} collective-permute-done((bf16[128,1280]{1,0:T(8,128)(2,1)S(1)}, bf16[128,1280]{1,0:T(8,128)(2,1)S(1)}, u32[]{:S(2)}, u32[]{:S(2)}) %collective-permute-start) | collective-permute-done | bytes 327712 | tf_op jit(solution)/shard_map/ppermute | solution.py:150
  40.9 1.2 add_convert_fusion.1
  42.1 4.4 %collective-permute-start.1 = (bf16[128,1280]{1,0:T(8,128)(2,1)S(1)}, bf16[128,1280]{1,0:T(8,128)(2,1)S(1)}, u32[]{:S(2)}, u32[]{:S(2)}) collective-permute-start(bf16[128,1280]{1,0:T(8,128)(2,1)S(1)} %add_convert_fusion.1), channel_id=1, source_target_pairs={{0,8},{8,16},{16,24},{1,9},{9,17},{17,25},{2,10},{10,18},{18,26},{... | collective-permute-start | bytes 983048 | tf_op jit(solution)/shard_map/ppermute | solution.py:150
  46.5 0.7 broadcast_in_dim_reshape.3.skip_ref
  47.2 5.3 %collective-permute-done.1 = bf16[128,1280]{1,0:T(8,128)(2,1)S(1)} collective-permute-done((bf16[128,1280]{1,0:T(8,128)(2,1)S(1)}, bf16[128,1280]{1,0:T(8,128)(2,1)S(1)}, u32[]{:S(2)}, u32[]{:S(2)}) %collective-permute-start.1) | collective-permute-done | bytes 327712 | tf_op jit(solution)/shard_map/ppermute | solution.py:150
  52.5 1.2 add_convert_fusion
  53.7 4.4 %collective-permute-start.2 = (bf16[128,1280]{1,0:T(8,128)(2,1)S(1)}, bf16[128,1280]{1,0:T(8,128)(2,1)S(1)}, u32[]{:S(2)}, u32[]{:S(2)}) collective-permute-start(bf16[128,1280]{1,0:T(8,128)(2,1)S(1)} %add_convert_fusion), channel_id=1, source_target_pairs={{0,8},{8,16},{16,24},{1,9},{9,17},{17,25},{2,10},{10,18},{18,26},{... | collective-permute-start | bytes 983048 | tf_op jit(solution)/shard_map/ppermute | solution.py:150
  58.1 19.3 %within.1.y_ref = bf16[2048,1280]{1,0:T(8,128)(2,1)} custom-call(s32[1]{0:T(128)} %bitcast.at_ref, bf16[2048,1280]{1,0:T(8,128)(2,1)} %x_ref.3, bf16[2048,1024]{1,0:T(8,128)(2,1)} %b_ref.3, bf16[2048,1024]{1,0:T(8,128)(2,1)} %c_ref.5, f32[20,2048]{1,0:T(8,128)} %step_ref.3, f32[20,2048]{1,0:T(8,128)} %log_ref.7, f32[1,1280]{1,0:T(1,128)} %broadcast_in_dim_reshape.3.skip_ref, ...), custom_call_target="tpu_custom_call" | custom-call | flops 10737418240 | bytes 20971520 | tf_op jit(solution)/shard_map/within/pallas_call | solution.py:210
  77.4 0.8 dynamic_slice.3
  78.8 0.7 copy-done.1
  79.5 20.0 %finish.3 = (bf16[1024,2560]{1,0:T(8,128)(2,1)}, f32[8,1024]{1,0:T(8,128)}) custom-call(s32[1]{0:T(128)} %bitcast.at_ref, bf16[2048,1280]{1,0:T(8,128)(2,1)} %within.1.y_ref, bf16[2048,1280]{1,0:T(8,128)(2,1)} %gate_ref.3, bf16[2048,1024]{1,0:T(8,128)(2,1)} %c_ref.5, f32[20,2048]{1,0:T(8,128)} %log_ref.7, f32[8,8,1280]{2,1,0:T(8,128)} %get-tuple-element.14.base_ref, ...), custom_call_target="tpu_custom_call" | custom-call | flops 6710886400 | bytes 17039360 | tf_op jit(solution)/shard_map/finish/pallas_call | solution.py:241
  99.5 20.0 %finish.2 = (bf16[1024,2560]{1,0:T(8,128)(2,1)}, f32[8,1024]{1,0:T(8,128)}) custom-call(s32[1]{0:T(128)} %bitcast.at_ref, bf16[2048,1280]{1,0:T(8,128)(2,1)} %within.1.y_ref, bf16[2048,1280]{1,0:T(8,128)(2,1)} %gate_ref.3, bf16[2048,1024]{1,0:T(8,128)(2,1)} %c_ref.5, f32[20,2048]{1,0:T(8,128)} %log_ref.7, f32[8,8,1280]{2,1,0:T(8,128)} %get-tuple-element.14.base_ref, ...), custom_call_target="tpu_custom_call" | custom-call | flops 6710886400 | bytes 17039360 | tf_op jit(solution)/shard_map/finish/pallas_call | solution.py:241
  119.5 0.6 copy-done.2
  120.7 0.8 slice_reduce_fusion.1
  121.5 0.8 slice_reduce_fusion.2
  122.3 10.8 %all-reduce = f32[4,512]{1,0:T(4,128)S(1)} all-reduce(f32[4,512]{1,0:T(4,128)S(1)} %pad_maximum_fusion), channel_id=4, replica_groups=mesh['seq'=4,'head'=4,'batch'=2] {'head'}, use_global_device_ids=true, to_apply=%region_2.3.clone | all-reduce | flops 2048 | bytes 16384
  133.2 0.7 fusion.1
  133.8 27.9 %reduce-scatter.5.cloned.1.call-done = bf16[256,2560]{1,0:T(8,128)(2,1)} async-done(((bf16[1024,2560]{1,0:T(8,128)(2,1)}), bf16[256,2560]{1,0:T(8,128)(2,1)}) %reduce-scatter.5.cloned.1.call-update) | async-done | bytes 1310736 | tf_op jit(solution)/shard_map/reduce_scatter | solution.py:274
  161.7 64.3 %reduce-scatter.3.cloned.1.call-done = bf16[256,2560]{1,0:T(8,128)(2,1)} async-done(((bf16[1024,2560]{1,0:T(8,128)(2,1)}), bf16[256,2560]{1,0:T(8,128)(2,1)}) %reduce-scatter.3.cloned.1.call-update) | async-done | bytes 1310736 | tf_op jit(solution)/shard_map/reduce_scatter | solution.py:274
  226.0 3.7 %multiply_convert_fusion = bf16[512,2560]{1,0:T(8,128)(2,1)} fusion(bf16[256,2560]{1,0:T(8,128)(2,1)} %reduce-scatter.5.cloned.1.call-done, bf16[256,2560]{1,0:T(8,128)(2,1)} %reduce-scatter.3.cloned.1.call-done, f32[512]{0:T(512)S(1)} %bitcast.3), kind=kLoop, calls=%fused_computation | loop fusion | flops 7864320 | bytes 5244928 | tf_op jit(solution)/shard_map/convert_element_type | solution.py:280
  (15 shorter events, 1.4 us)
Async XLA Ops:
  6.5 155.2 %reduce-scatter.5.cloned.1.call-start = ((), (), s32[]{:S(2)}) async-start(), calls=%async_computation.3 | async-start | bytes 6553600 | tf_op jit(solution)/shard_map/reduce_scatter | solution.py:274
  6.5 39.9 %copy-start = (f32[20]{0:T(128)S(1)}, f32[20]{0:T(128)}, u32[]{:S(2)}) copy-start(f32[20]{0:T(128)} %param.15) | copy-start | bytes 244
  29.0 11.9 %collective-permute-start = (bf16[128,1280]{1,0:T(8,128)(2,1)S(1)}, bf16[128,1280]{1,0:T(8,128)(2,1)S(1)}, u32[]{:S(2)}, u32[]{:S(2)}) collective-permute-start(bf16[128,1280]{1,0:T(8,128)(2,1)S(1)} %convert_element_type.21), channel_id=1, source_target_pairs={{0,8},{8,16},{16,24},{1,9},{9,17},{17,25},{2,10},{10,18},{18,26},{... | collective-permute-start | bytes 983048 | tf_op jit(solution)/shard_map/ppermute | solution.py:150
  42.1 10.5 %collective-permute-start.1 = (bf16[128,1280]{1,0:T(8,128)(2,1)S(1)}, bf16[128,1280]{1,0:T(8,128)(2,1)S(1)}, u32[]{:S(2)}, u32[]{:S(2)}) collective-permute-start(bf16[128,1280]{1,0:T(8,128)(2,1)S(1)} %add_convert_fusion.1), channel_id=1, source_target_pairs={{0,8},{8,16},{16,24},{1,9},{9,17},{17,25},{2,10},{10,18},{18,26},{... | collective-permute-start | bytes 983048 | tf_op jit(solution)/shard_map/ppermute | solution.py:150
  53.7 25.1 %collective-permute-start.2 = (bf16[128,1280]{1,0:T(8,128)(2,1)S(1)}, bf16[128,1280]{1,0:T(8,128)(2,1)S(1)}, u32[]{:S(2)}, u32[]{:S(2)}) collective-permute-start(bf16[128,1280]{1,0:T(8,128)(2,1)S(1)} %add_convert_fusion), channel_id=1, source_target_pairs={{0,8},{8,16},{16,24},{1,9},{9,17},{17,25},{2,10},{10,18},{18,26},{... | collective-permute-start | bytes 983048 | tf_op jit(solution)/shard_map/ppermute | solution.py:150
  78.8 0.7 copy-start.1
  99.5 126.6 %reduce-scatter.3.cloned.1.call-start = ((), (), s32[]{:S(2)}) async-start(), calls=%async_computation.2 | async-start | bytes 6553600 | tf_op jit(solution)/shard_map/reduce_scatter | solution.py:274
  119.5 0.7 copy-start.2
Sparse Core Ops, SparseCore 0:
  99.6 62.0 reduce-scatter.4
  164.7 61.3 reduce-scatter.2
where the time goes:
time: 237 us
  waiting for transfers between devices  104 us (44%)
  Pallas kernels  80.5 us (34%)
  starting transfers between devices  13.8 us (6%)
  between operations  13.5 us (6%)
  blocking collectives  10.8 us (5%)
  other arithmetic  7.81 us (3%)
  local copies, waits for them, and re-layouts  6.41 us (3%)
    reduce_scatter x2, waiting for transfers between devices, body(): lax.psum_scatter(partial, 'head', scatter_dimension=0, tiled=True)  92.2 us
    pallas_call x2, Pallas kernels, body(): pl.pallas_call(functools.partial(finish_kernel, repeats), grid_spec=pltpu...  39.9 us
    pallas_call x1, Pallas kernels, body(): pl.pallas_call(functools.partial(state_kernel, repeats), grid_spec=pltpu....  21.3 us
    pallas_call x1, Pallas kernels, body(): pl.pallas_call(functools.partial(within_kernel, repeats), grid_spec=pltpu...  19.3 us
    ppermute x3, starting transfers between devices, shifted(): lax.ppermute(value, axis, [(source, source + steps) for source in range(c...  13.8 us
    ppermute x3, waiting for transfers between devices, shifted(): lax.ppermute(value, axis, [(source, source + steps) for source in range(c...  11.5 us
    unnamed x1, blocking collectives  10.8 us
  transfers between devices with their start and end apart: 5, of which 4 were waited for; matrix products, arithmetic and copies ran while one was open for 2% of the time, Pallas kernels for 17%

commit v1 on v0

--- a/solution.py
+++ b/solution.py
@@ -207,30 +207,6 @@
     for _ in range(lax.axis_size("seq") - 2):
         incoming = shifted((decay[0:1] * incoming.astype(F32) + total).astype(BF16), "seq", 1)
 
-    y = pl.pallas_call(
-        functools.partial(within_kernel, repeats),
-        grid_spec=pltpu.PrefetchScalarGridSpec(
-            num_scalar_prefetch=1,
-            grid=(blocks,),
-            in_specs=[
-                rows_of(channels),
-                grouped,
-                grouped,
-                head_rows,
-                head_rows,
-                fixed(1, channels),
-                state_block,
-            ],
-            out_specs=rows_of(channels),
-        ),
-        out_shape=jax.ShapeDtypeStruct((tokens, channels), BF16),
-        compiler_params=params,
-        name="within",
-        cost_estimate=pl.CostEstimate(
-            flops=16 * tokens * channels * BLOCK, bytes_accessed=tokens * channels * 8, transcendentals=0
-        ),
-    )(at, ssm_input, b_proj, c_proj, step_size, log_decay, skip, prefix)
-
     shares = lax.axis_size("head")
     per_share = tokens // shares
     chunks = max(1, per_share // BLOCK)
@@ -238,14 +214,38 @@
     parts, squares = [], []
     for chunk in range(chunks):
         pick = lambda d, chunk=chunk: d * chunks + chunk
+        picked = lambda width, pick=pick: pl.BlockSpec((BLOCK, width), lambda d, at: (pick(d), 0))
+        y = pl.pallas_call(
+            functools.partial(within_kernel, repeats),
+            grid_spec=pltpu.PrefetchScalarGridSpec(
+                num_scalar_prefetch=1,
+                grid=(steps,),
+                in_specs=[
+                    picked(channels),
+                    pl.BlockSpec((BLOCK, groups * STATE), lambda d, at: (pick(d), at[0])),
+                    pl.BlockSpec((BLOCK, groups * STATE), lambda d, at: (pick(d), at[0])),
+                    pl.BlockSpec((heads, BLOCK), lambda d, at: (0, pick(d))),
+                    pl.BlockSpec((heads, BLOCK), lambda d, at: (0, pick(d))),
+                    fixed(1, channels),
+                    pl.BlockSpec((1, STATE, channels), lambda d, at: (pick(d), 0, 0)),
+                ],
+                out_specs=rows_of(channels),
+            ),
+            out_shape=jax.ShapeDtypeStruct((steps * BLOCK, channels), BF16),
+            compiler_params=params,
+            name="within",
+            cost_estimate=pl.CostEstimate(
+                flops=16 * steps * BLOCK * channels * BLOCK, bytes_accessed=steps * BLOCK * channels * 8, transcendentals=0
+            ),
+        )(at, ssm_input, b_proj, c_proj, step_size, log_decay, skip, prefix)
         partial, square = pl.pallas_call(
             functools.partial(finish_kernel, repeats),
             grid_spec=pltpu.PrefetchScalarGridSpec(
                 num_scalar_prefetch=1,
                 grid=(steps,),
                 in_specs=[
-                    pl.BlockSpec((BLOCK, channels), lambda d, at: (pick(d), 0)),
-                    pl.BlockSpec((BLOCK, channels), lambda d, at: (pick(d), 0)),
+                    rows_of(channels),
+                    picked(channels),
                     pl.BlockSpec((BLOCK, groups * STATE), lambda d, at: (pick(d), at[0])),
                     pl.BlockSpec((heads, BLOCK), lambda d, at: (0, pick(d))),
                     pl.BlockSpec((1, 8, channels), lambda d, at: (pick(d), 0, 0)),

time: 237 us -> 227 us (0.958)
  waiting for transfers between devices: 104 us -> 91.6 us
    reduce_scatter x2, waiting for transfers between devices: 92.2 us -> 81.5 us  [body(): lax.psum_scatter(partial, 'head', scatter_dimension=0, tiled=True)]
    pallas_call x1 -> x2, Pallas kernels: 19.3 us -> 21.5 us  [body(): pl.pallas_call(functools.partial(within_kernel, repeats), grid_spec=pltpu...]
  transfers between devices with their start and end apart: 5 -> 5, of which waited for: 4 -> 4; matrix products, arithmetic and copies ran while one was open for 2% -> 3% of each run, Pallas kernels for 17% -> 18%
where the time goes in v1:
time: 227 us
  waiting for transfers between devices  91.6 us (40%)
  Pallas kernels  82.7 us (36%)
  starting transfers between devices  14 us (6%)
  between operations  13.5 us (6%)
  blocking collectives  10.3 us (5%)
  other arithmetic  7.84 us (3%)
  local copies, waits for them, and re-layouts  6.51 us (3%)
    reduce_scatter x2, waiting for transfers between devices, body(): lax.psum_scatter(partial, 'head', scatter_dimension=0, tiled=True)  81.5 us
    pallas_call x2, Pallas kernels, body(): pl.pallas_call(functools.partial(finish_kernel, repeats), grid_spec=pltpu...  40 us
    pallas_call x2, Pallas kernels, body(): pl.pallas_call(functools.partial(within_kernel, repeats), grid_spec=pltpu...  21.5 us
    pallas_call x1, Pallas kernels, body(): pl.pallas_call(functools.partial(state_kernel, repeats), grid_spec=pltpu....  21.3 us
    ppermute x3, starting transfers between devices, shifted(): lax.ppermute(value, axis, [(source, source + steps) for source in range(c...  13.8 us
    unnamed x1, blocking collectives  10.3 us
    ppermute x3, waiting for transfers between devices, shifted(): lax.ppermute(value, axis, [(source, source + steps) for source in range(c...  10.1 us
  transfers between devices with their start and end apart: 5, of which 4 were waited for; matrix products, arithmetic and copies ran while one was open for 3% of the time, Pallas kernels for 18%

profile of v1, /device:TPU:0, one launch (start us, length us, event | category | flops | bytes accessed | tf_op | source)
XLA Modules:
  0.0 226.5 jit_solution(18260190997612217312)
XLA Ops:
  6.5 21.3 %block_states.1 = (bf16[8,128,1280]{2,1,0:T(8,128)(2,1)}, f32[8,8,1280]{2,1,0:T(8,128)}, f32[128,1280]{1,0:T(8,128)}, f32[8,1280]{1,0:T(8,128)}) custom-call(s32[1]{0:T(128)} %bitcast.at_ref, bf16[2048,1280]{1,0:T(8,128)(2,1)} %x_ref.5, bf16[2048,1024]{1,0:T(8,128)(2,1)} %b_ref.5, f32[20,2048]{1,0:T(8,128)} %step_ref.5, f32[20,2048]{1,0:T(8,128)} %log_ref.9), custom_call_target="tpu_custom_call" | custom-call | flops 671088640 | bytes 10485760 | tf_op jit(solution)/shard_map/block_states/pallas_call | solution.py:179
  27.8 1.1 convert_element_type.21
  29.0 5.0 %collective-permute-start = (bf16[128,1280]{1,0:T(8,128)(2,1)S(1)}, bf16[128,1280]{1,0:T(8,128)(2,1)S(1)}, u32[]{:S(2)}, u32[]{:S(2)}) collective-permute-start(bf16[128,1280]{1,0:T(8,128)(2,1)S(1)} %convert_element_type.21), channel_id=1, source_target_pairs={{0,8},{8,16},{16,24},{1,9},{9,17},{17,25},{2,10},{10,18},{18,26},{... | collective-permute-start | bytes 983048 | tf_op jit(solution)/shard_map/ppermute | solution.py:150
  34.0 0.8 slice_reduce_fusion
  34.8 6.1 %collective-permute-done = bf16[128,1280]{1,0:T(8,128)(2,1)S(1)} collective-permute-done((bf16[128,1280]{1,0:T(8,128)(2,1)S(1)}, bf16[128,1280]{1,0:T(8,128)(2,1)S(1)}, u32[]{:S(2)}, u32[]{:S(2)}) %collective-permute-start) | collective-permute-done | bytes 327712 | tf_op jit(solution)/shard_map/ppermute | solution.py:150
  40.9 1.2 add_convert_fusion.1
  42.1 4.4 %collective-permute-start.1 = (bf16[128,1280]{1,0:T(8,128)(2,1)S(1)}, bf16[128,1280]{1,0:T(8,128)(2,1)S(1)}, u32[]{:S(2)}, u32[]{:S(2)}) collective-permute-start(bf16[128,1280]{1,0:T(8,128)(2,1)S(1)} %add_convert_fusion.1), channel_id=1, source_target_pairs={{0,8},{8,16},{16,24},{1,9},{9,17},{17,25},{2,10},{10,18},{18,26},{... | collective-permute-start | bytes 983048 | tf_op jit(solution)/shard_map/ppermute | solution.py:150
  46.5 0.8 dynamic_slice.3
  47.9 0.7 broadcast_in_dim_reshape.3.skip_ref
  48.6 3.9 %collective-permute-done.1 = bf16[128,1280]{1,0:T(8,128)(2,1)S(1)} collective-permute-done((bf16[128,1280]{1,0:T(8,128)(2,1)S(1)}, bf16[128,1280]{1,0:T(8,128)(2,1)S(1)}, u32[]{:S(2)}, u32[]{:S(2)}) %collective-permute-start.1) | collective-permute-done | bytes 327712 | tf_op jit(solution)/shard_map/ppermute | solution.py:150
  52.5 1.2 add_convert_fusion
  53.7 4.4 %collective-permute-start.2 = (bf16[128,1280]{1,0:T(8,128)(2,1)S(1)}, bf16[128,1280]{1,0:T(8,128)(2,1)S(1)}, u32[]{:S(2)}, u32[]{:S(2)}) collective-permute-start(bf16[128,1280]{1,0:T(8,128)(2,1)S(1)} %add_convert_fusion), channel_id=1, source_target_pairs={{0,8},{8,16},{16,24},{1,9},{9,17},{17,25},{2,10},{10,18},{18,26},{... | collective-permute-start | bytes 983048 | tf_op jit(solution)/shard_map/ppermute | solution.py:150
  58.1 10.7 %within.2.y_ref = bf16[1024,1280]{1,0:T(8,128)(2,1)} custom-call(s32[1]{0:T(128)} %bitcast.at_ref, bf16[2048,1280]{1,0:T(8,128)(2,1)} %x_ref.5, bf16[2048,1024]{1,0:T(8,128)(2,1)} %b_ref.5, bf16[2048,1024]{1,0:T(8,128)(2,1)} %c_ref.7, f32[20,2048]{1,0:T(8,128)} %step_ref.5, f32[20,2048]{1,0:T(8,128)} %log_ref.9, f32[1,1280]{1,0:T(1,128)} %broadcast_in_dim_reshape.3.skip_ref, ...), custom_call_target="tpu_custom_call" | custom-call | flops 5368709120 | bytes 10485760 | tf_op jit(solution)/shard_map/within/pallas_call | solution.py:218
  68.9 0.7 copy-done.1
  69.6 19.9 %finish.2 = (bf16[1024,2560]{1,0:T(8,128)(2,1)}, f32[8,1024]{1,0:T(8,128)}) custom-call(s32[1]{0:T(128)} %bitcast.at_ref, bf16[1024,1280]{1,0:T(8,128)(2,1)} %within.2.y_ref, bf16[2048,1280]{1,0:T(8,128)(2,1)} %gate_ref.3, bf16[2048,1024]{1,0:T(8,128)(2,1)} %c_ref.7, f32[20,2048]{1,0:T(8,128)} %log_ref.9, f32[8,8,1280]{2,1,0:T(8,128)} %get-tuple-element.14.base_ref, ...), custom_call_target="tpu_custom_call" | custom-call | flops 6710886400 | bytes 17039360 | tf_op jit(solution)/shard_map/finish/pallas_call | solution.py:241
  89.8 10.7 %within.3.y_ref = bf16[1024,1280]{1,0:T(8,128)(2,1)} custom-call(s32[1]{0:T(128)} %bitcast.at_ref, bf16[2048,1280]{1,0:T(8,128)(2,1)} %x_ref.5, bf16[2048,1024]{1,0:T(8,128)(2,1)} %b_ref.5, bf16[2048,1024]{1,0:T(8,128)(2,1)} %c_ref.7, f32[20,2048]{1,0:T(8,128)} %step_ref.5, f32[20,2048]{1,0:T(8,128)} %log_ref.9, f32[1,1280]{1,0:T(1,128)} %broadcast_in_dim_reshape.3.skip_ref, ...), custom_call_target="tpu_custom_call" | custom-call | flops 5368709120 | bytes 10485760 | tf_op jit(solution)/shard_map/within/pallas_call | solution.py:218
  100.6 20.0 %finish.3 = (bf16[1024,2560]{1,0:T(8,128)(2,1)}, f32[8,1024]{1,0:T(8,128)}) custom-call(s32[1]{0:T(128)} %bitcast.at_ref, bf16[1024,1280]{1,0:T(8,128)(2,1)} %within.3.y_ref, bf16[2048,1280]{1,0:T(8,128)(2,1)} %gate_ref.3, bf16[2048,1024]{1,0:T(8,128)(2,1)} %c_ref.7, f32[20,2048]{1,0:T(8,128)} %log_ref.9, f32[8,8,1280]{2,1,0:T(8,128)} %get-tuple-element.14.base_ref, ...), custom_call_target="tpu_custom_call" | custom-call | flops 6710886400 | bytes 17039360 | tf_op jit(solution)/shard_map/finish/pallas_call | solution.py:241
  121.9 0.8 slice_reduce_fusion.2
  122.7 0.8 slice_reduce_fusion.1
  123.5 10.3 %all-reduce = f32[4,512]{1,0:T(4,128)S(1)} all-reduce(f32[4,512]{1,0:T(4,128)S(1)} %pad_maximum_fusion), channel_id=4, replica_groups=mesh['seq'=4,'head'=4,'batch'=2] {'head'}, use_global_device_ids=true, to_apply=%region_2.3.clone | all-reduce | flops 2048 | bytes 16384
  133.8 0.7 fusion.1
  134.5 17.2 %reduce-scatter.3.cloned.1.call-done = bf16[256,2560]{1,0:T(8,128)(2,1)} async-done(((bf16[1024,2560]{1,0:T(8,128)(2,1)}), bf16[256,2560]{1,0:T(8,128)(2,1)}) %reduce-scatter.3.cloned.1.call-update) | async-done | bytes 1310736 | tf_op jit(solution)/shard_map/reduce_scatter | solution.py:274
  151.6 64.3 %reduce-scatter.5.cloned.1.call-done = bf16[256,2560]{1,0:T(8,128)(2,1)} async-done(((bf16[1024,2560]{1,0:T(8,128)(2,1)}), bf16[256,2560]{1,0:T(8,128)(2,1)}) %reduce-scatter.5.cloned.1.call-update) | async-done | bytes 1310736 | tf_op jit(solution)/shard_map/reduce_scatter | solution.py:274
  216.0 3.7 %multiply_convert_fusion = bf16[512,2560]{1,0:T(8,128)(2,1)} fusion(bf16[256,2560]{1,0:T(8,128)(2,1)} %reduce-scatter.5.cloned.1.call-done, bf16[256,2560]{1,0:T(8,128)(2,1)} %reduce-scatter.3.cloned.1.call-done, f32[512]{0:T(512)S(1)} %bitcast.3), kind=kLoop, calls=%fused_computation | loop fusion | flops 7864320 | bytes 5244928 | tf_op jit(solution)/shard_map/convert_element_type | solution.py:280
  (16 shorter events, 2.2 us)
Async XLA Ops:
  6.5 145.1 %reduce-scatter.3.cloned.1.call-start = ((), (), s32[]{:S(2)}) async-start(), calls=%async_computation.2 | async-start | bytes 6553600 | tf_op jit(solution)/shard_map/reduce_scatter | solution.py:274
  6.5 41.3 %copy-start = (f32[20]{0:T(128)S(1)}, f32[20]{0:T(128)}, u32[]{:S(2)}) copy-start(f32[20]{0:T(128)} %param.15) | copy-start | bytes 244
  29.0 11.9 %collective-permute-start = (bf16[128,1280]{1,0:T(8,128)(2,1)S(1)}, bf16[128,1280]{1,0:T(8,128)(2,1)S(1)}, u32[]{:S(2)}, u32[]{:S(2)}) collective-permute-start(bf16[128,1280]{1,0:T(8,128)(2,1)S(1)} %convert_element_type.21), channel_id=1, source_target_pairs={{0,8},{8,16},{16,24},{1,9},{9,17},{17,25},{2,10},{10,18},{18,26},{... | collective-permute-start | bytes 983048 | tf_op jit(solution)/shard_map/ppermute | solution.py:150
  42.1 10.5 %collective-permute-start.1 = (bf16[128,1280]{1,0:T(8,128)(2,1)S(1)}, bf16[128,1280]{1,0:T(8,128)(2,1)S(1)}, u32[]{:S(2)}, u32[]{:S(2)}) collective-permute-start(bf16[128,1280]{1,0:T(8,128)(2,1)S(1)} %add_convert_fusion.1), channel_id=1, source_target_pairs={{0,8},{8,16},{16,24},{1,9},{9,17},{17,25},{2,10},{10,18},{18,26},{... | collective-permute-start | bytes 983048 | tf_op jit(solution)/shard_map/ppermute | solution.py:150
  53.7 15.2 %collective-permute-start.2 = (bf16[128,1280]{1,0:T(8,128)(2,1)S(1)}, bf16[128,1280]{1,0:T(8,128)(2,1)S(1)}, u32[]{:S(2)}, u32[]{:S(2)}) collective-permute-start(bf16[128,1280]{1,0:T(8,128)(2,1)S(1)} %add_convert_fusion), channel_id=1, source_target_pairs={{0,8},{8,16},{16,24},{1,9},{9,17},{17,25},{2,10},{10,18},{18,26},{... | collective-permute-start | bytes 983048 | tf_op jit(solution)/shard_map/ppermute | solution.py:150
  68.9 0.8 copy-start.1
  89.6 126.4 %reduce-scatter.5.cloned.1.call-start = ((), (), s32[]{:S(2)}) async-start(), calls=%async_computation.3 | async-start | bytes 6553600 | tf_op jit(solution)/shard_map/reduce_scatter | solution.py:274
  120.6 0.7 copy-start.2
Sparse Core Ops, SparseCore 0:
  89.7 61.8 reduce-scatter.2
  154.6 61.3 reduce-scatter.4
